TPU v7x, 32 devices: a whole 2x2x4 slice. The times are simulated.
32 devices in a mesh: morton: 8 (over z, x), level: 4 (over y, core).
Axes of the slice: x: 2, y: 2, z: 4, core: 2. Of those that a mesh axis runs over, the one named last changes fastest.
Arguments:
- coarse_density: float32 [4096, 128], P('morton'), may hold values from 0.000125 to 0.12
- coarse_emission: float32 [4096, 128], P('morton'), may hold values from 0 to 4
- fine_density: float32 [16384, 128], P(('morton', 'level')), may hold values from 0.000125 to 0.12
- fine_emission: float32 [16384, 128], P(('morton', 'level')), may hold values from 0 to 4
- coarse_brick: int32 [32768], P(('morton', 'level')), may hold values from 0 to 15
- coarse_lane: int32 [32768], P(('morton', 'level')), may hold values from 0 to 1023
- coarse_entry: int32 [32768], P(('morton', 'level')), may hold values from 0 to 31, as said below
- coarse_count: int32 [32768], P(('morton', 'level')), may hold values from 0 to 32, as said below
- fine_owner: int32 [262144, 1], P(('morton', 'level')), may hold values from 0 to 31; in each aligned block of 8192 rows (0 to 8191, 8192 to 16383, ...) at most 512 rows name the same one
- fine_brick: int32 [262144], P(('morton', 'level')), may hold values from 0 to 1
- fine_lane: int32 [262144], P(('morton', 'level')), may hold values from 0 to 1023
- fine_entry: int32 [262144], P(('morton', 'level')), may hold values from 0 to 31, as said below
- fine_count: int32 [262144], P(('morton', 'level')), may hold values from 0 to 32, as said below
Outputs:
- image_color: float32 [8192], P(('morton', 'level'))
- transmittance: float32 [8192], P(('morton', 'level'))
Inputs may be any that keep to these rules, and one draw needn't show every extreme that they name: `coarse_entry`: entry plus count is at most 32 for each segment. `coarse_count`: count 0 marks an empty segment. `fine_entry`: entry plus count is at most 32 for each segment. `fine_count`: count 0 marks a padded slot. `fine_owner`: among the fine segments of one device, at most 512 name one owner device, a bound that some block reaches.
All inputs are finite; a program needn't handle non-finite values.
Results may differ from a plain program's by a relative error of at most 0.0003.
Values sent between devices are 32-bit elements; how exact they have to be, the bound alone decides.
No kernel may reach another device: no remote copies, remote signals or barrier semaphores. Data moves between devices by JAX's collectives and lax.ppermute only.
A program may use at most 64 MiB of HBM per device.

v0:
```python
import math

import jax
import jax.numpy as jnp
from jax import lax
from jax.sharding import PartitionSpec as P

BRICK = 32


def march(density_rows, emission_rows, lane_ids, entry_ids, count_ids):
    per_row = 128 // BRICK
    chosen = ((lane_ids % per_row)[:, None] == lax.broadcasted_iota(jnp.int32, (1, per_row), 1))[
        :, :, None
    ]
    nothing = jnp.float32(0.0)
    dens_lane = jnp.sum(
        jnp.where(chosen, density_rows.reshape(-1, per_row, BRICK), nothing), axis=1
    ).T
    emis_lane = jnp.sum(
        jnp.where(chosen, emission_rows.reshape(-1, per_row, BRICK), nothing), axis=1
    ).T
    step_ids = lax.broadcasted_iota(jnp.int32, (BRICK, 1), 0)
    inside = (step_ids >= entry_ids[None, :]) & (step_ids < (entry_ids + count_ids)[None, :])
    optical = jnp.where(inside, dens_lane, nothing)
    before = jnp.cumsum(optical, axis=0) - optical
    opacity = 1.0 - jnp.exp(-optical)
    colors = jnp.sum(jnp.exp(-before) * opacity * emis_lane, axis=0)
    return (colors, jnp.sum(optical, axis=0))


def sample_table(dens_table, emis_table, brick_ids, lane_ids, entry_ids, count_ids):
    total = brick_ids.shape[0]
    block_size = math.gcd(total, 2048)
    brick_rows = BRICK**3 // 128

    def sample_one_block(inputs):
        b_ids, l_ids, e_ids, c_ids = inputs
        row_index = b_ids * brick_rows + l_ids // (128 // BRICK)
        return march(dens_table[row_index], emis_table[row_index], l_ids, e_ids, c_ids)

    shaped = tuple(
        (
            item.reshape(total // block_size, block_size)
            for item in (brick_ids, lane_ids, entry_ids, count_ids)
        )
    )
    colors, depths = lax.map(sample_one_block, shaped)
    return (colors.reshape(total), depths.reshape(total))


def encode_record(brick_ids, lane_ids, entry_ids, count_ids):
    return ((brick_ids * (BRICK * BRICK) + lane_ids) * BRICK + entry_ids) * (BRICK + 1) + count_ids


def decode_record(codes):
    count_ids = codes % (BRICK + 1)
    rest = codes // (BRICK + 1)
    entry_ids = rest % BRICK
    rest = rest // BRICK
    lane_ids = rest % (BRICK * BRICK)
    brick_ids = rest // (BRICK * BRICK)
    return (brick_ids, lane_ids, entry_ids, count_ids)


def serve_codes(dens_table, emis_table, codes):
    b_ids, l_ids, e_ids, c_ids = decode_record(codes.reshape(-1))
    colors, depths = sample_table(dens_table, emis_table, b_ids, l_ids, e_ids, c_ids)
    return (colors.reshape(codes.shape), depths.reshape(codes.shape))


def slot_ranks(target, width):
    total = target.shape[0]
    block_size = math.gcd(total, 2048)
    columns = lax.broadcasted_iota(jnp.int32, (1, width), 1)

    def slot_one_block(offsets, block):
        onehot = (block[:, None] == columns).astype(jnp.int32)
        within = jnp.cumsum(onehot, axis=0) - onehot
        ranks = jnp.sum((within + offsets[None, :]) * onehot, axis=1)
        return (offsets + jnp.sum(onehot, axis=0), ranks)

    start = jnp.zeros((width,), jnp.int32)
    unused, ranks = lax.scan(slot_one_block, start, target.reshape(total // block_size, block_size))
    return ranks.reshape(total)


def shards(
    coarse_density,
    coarse_emission,
    fine_density,
    fine_emission,
    coarse_brick,
    coarse_lane,
    coarse_entry,
    coarse_count,
    fine_owner,
    fine_brick,
    fine_lane,
    fine_entry,
    fine_count,
):
    n_morton = lax.axis_size("morton")
    n_level = lax.axis_size("level")
    segments = fine_brick.shape[0]
    pixels = coarse_brick.shape[0]
    route_cap = 2 * segments // (n_morton * n_level)
    owner = fine_owner[:, 0]
    own_bricks = fine_density.shape[0] // (BRICK**3 // 128)
    coarse_dens, coarse_emis = (
        lax.all_gather(coarse_density, "morton", axis=0, tiled=True),
        lax.all_gather(coarse_emission, "morton", axis=0, tiled=True),
    )
    group_dens, group_emis = (
        lax.all_gather(fine_density, "level", axis=0, tiled=True),
        lax.all_gather(fine_emission, "level", axis=0, tiled=True),
    )
    target = owner // n_level
    capacity = n_level * route_cap
    local_brick = owner % n_level * own_bricks + fine_brick
    ranks = slot_ranks(target, n_morton)
    destination = target * capacity + ranks
    codes = encode_record(local_brick, fine_lane, fine_entry, fine_count)
    buffer = jnp.zeros((n_morton * capacity,), jnp.int32).at[destination].set(codes)
    coarse_color, coarse_depth = sample_table(
        coarse_dens, coarse_emis, coarse_brick, coarse_lane, coarse_entry, coarse_count
    )
    requests = buffer.reshape(n_morton, capacity)
    shaped = serve_codes(
        group_dens,
        group_emis,
        lax.all_to_all(requests, "morton", split_axis=0, concat_axis=0, tiled=True),
    )
    colors_back = lax.all_to_all(shaped[0], "morton", split_axis=0, concat_axis=0, tiled=True)
    depths_back = lax.all_to_all(shaped[1], "morton", split_axis=0, concat_axis=0, tiled=True)
    seg_color = colors_back.reshape(-1)[destination].reshape(pixels, -1)
    seg_depth = depths_back.reshape(-1)[destination].reshape(pixels, -1)
    earlier = jnp.cumsum(seg_depth, axis=1) - seg_depth
    slab_color = coarse_color + jnp.exp(-coarse_depth) * jnp.sum(
        jnp.exp(-earlier) * seg_color, axis=1
    )
    slab_depth = coarse_depth + jnp.sum(seg_depth, axis=1)
    quarter = pixels // n_level
    all_color, all_depth = (
        lax.all_gather(slab_color.reshape(1, pixels), "level", axis=0, tiled=True),
        lax.all_gather(slab_depth.reshape(1, pixels), "level", axis=0, tiled=True),
    )
    start = lax.axis_index("level") * quarter
    part_color = lax.dynamic_slice_in_dim(all_color, start, quarter, 1)
    part_depth = lax.dynamic_slice_in_dim(all_depth, start, quarter, 1)
    in_front = jnp.cumsum(part_depth, axis=0) - part_depth
    image_color = jnp.sum(jnp.exp(-in_front) * part_color, axis=0)
    transmittance = jnp.exp(-jnp.sum(part_depth, axis=0))
    return (image_color, transmittance)


def solution(mesh):
    return jax.shard_map(
        shards,
        mesh=mesh,
        in_specs=(
            P("morton", None),
            P("morton", None),
            P(("morton", "level"), None),
            P(("morton", "level"), None),
            P(("morton", "level")),
            P(("morton", "level")),
            P(("morton", "level")),
            P(("morton", "level")),
            P(("morton", "level"), None),
            P(("morton", "level")),
            P(("morton", "level")),
            P(("morton", "level")),
            P(("morton", "level")),
        ),
        out_specs=(P(("morton", "level")), P(("morton", "level"))),
        check_vma=False,
    )
```

profile of v0, /device:TPU:0, one launch (start us, length us, event | category | flops | bytes accessed | tf_op | source)
XLA Modules:
  0.0 336.4 jit_solution(13316824479454319103)
XLA Ops:
  10.0 1.4 reduce.5
  11.5 12.9 %while.36 = (s32[]{:T(128)}, s32[8]{0:T(128)S(1)}, s32[4,2048]{1,0:T(4,128)S(1)}, s32[4,2048]{1,0:T(4,128)S(1)}) while((s32[]{:T(128)}, s32[8]{0:T(128)S(1)}, s32[4,2048]{1,0:T(4,128)S(1)}, s32[4,2048]{1,0:T(4,128)S(1)}) %tuple.84), condition=%wide.region_7.8_spmd.clone.clone.clone, body=%wide.region_2.7_spmd.clone.clone.sunk.clone | while | flops 2244619 | bytes 453456 | solution.py:84
  11.6 2.3 reduce-window.18
  14.8 2.3 reduce-window.18
  18.0 2.3 reduce-window.18
  21.2 2.3 reduce-window.18
  24.8 31.0 %scatter_custom_fusion = s32[16384]{0:T(1024)} fusion(s32[8192]{0:T(1024)S(1)} %bitcast.178, s32[8192]{0:T(1024)S(1)} %fusion.27, s32[]{:T(128)} %copy.90), kind=kCustom, calls=%fused_computation.103 | custom fusion | bytes 65540 | tf_op jit(solution)/shard_map/scatter | solution.py:124
  55.8 7.3 %all-to-all-start = ((s32[8,1,2048]{2,1,0:T(1,128)}), s32[8,1,2048]{2,1,0:T(1,128)S(1)}, u32[]{:S(2)}, u32[]{:S(2)}) async-start(s32[8,1,2048]{2,1,0:T(1,128)} %bitcast.16), calls=%async_computation | async-start | bytes 131072 | tf_op jit(solution)/shard_map/all_to_all | solution.py:132
  63.7 7.0 %all-to-all-done = s32[8,1,2048]{2,1,0:T(1,128)S(1)} async-done(((s32[8,1,2048]{2,1,0:T(1,128)}), s32[8,1,2048]{2,1,0:T(1,128)S(1)}, u32[]{:S(2)}, u32[]{:S(2)}) %all-to-all-start) | async-done | bytes 65568 | tf_op jit(solution)/shard_map/all_to_all | solution.py:132
  71.1 129.9 %while.35 = (s32[]{:T(128)}, f32[8,2048]{1,0:T(8,128)S(1)}, f32[8,2048]{1,0:T(8,128)}, s32[8,2048]{1,0:T(8,128)S(1)}, s32[8,2048]{1,0:T(8,128)S(1)}, /*index=5*/...) while((s32[]{:T(128)}, f32[8,2048]{1,0:T(8,128)S(1)}, ...), condition=%wide.region_15.16_spmd.clone, body=%wide.region_9.15_spmd.sunk.clone | while | flops 4069378 | bytes 17268876 | solution.py:48
  71.3 6.7 %gather_fusion = f32[2048,128]{1,0:T(8,128)S(1)} fusion(f32[2048,128]{1,0:T(8,128)} %get-tuple-element.438, s32[2048]{0:T(1024)S(1)} %broadcast_clamp_fusion.4), kind=kCustom, calls=%fused_computation.clone.1.clone | custom fusion | bytes 2105344 | tf_op jit(solution)/shard_map/while/body/eval_jaxpr/gather | solution.py:40
  78.3 0.9 copy-done
  79.2 5.5 %gather_fusion.1 = f32[2048,128]{1,0:T(8,128)S(1)} fusion(f32[2048,128]{1,0:T(8,128)S(1)} %copy-done, s32[2048]{0:T(1024)S(1)} %broadcast_clamp_fusion.4), kind=kCustom, calls=%fused_computation.1.clone.1.clone | custom fusion | bytes 2105344 | tf_op jit(solution)/shard_map/while/body/eval_jaxpr/gather | solution.py:40
  85.7 1.5 dynamic_update_slice.31
  87.5 6.7 %gather_fusion = f32[2048,128]{1,0:T(8,128)S(1)} fusion(f32[2048,128]{1,0:T(8,128)} %get-tuple-element.438, s32[2048]{0:T(1024)S(1)} %broadcast_clamp_fusion.4), kind=kCustom, calls=%fused_computation.clone.1.clone | custom fusion | bytes 2105344 | tf_op jit(solution)/shard_map/while/body/eval_jaxpr/gather | solution.py:40
  94.5 0.9 copy-done
  95.4 5.5 %gather_fusion.1 = f32[2048,128]{1,0:T(8,128)S(1)} fusion(f32[2048,128]{1,0:T(8,128)S(1)} %copy-done, s32[2048]{0:T(1024)S(1)} %broadcast_clamp_fusion.4), kind=kCustom, calls=%fused_computation.1.clone.1.clone | custom fusion | bytes 2105344 | tf_op jit(solution)/shard_map/while/body/eval_jaxpr/gather | solution.py:40
  101.9 1.5 dynamic_update_slice.31
  103.7 6.7 %gather_fusion = f32[2048,128]{1,0:T(8,128)S(1)} fusion(f32[2048,128]{1,0:T(8,128)} %get-tuple-element.438, s32[2048]{0:T(1024)S(1)} %broadcast_clamp_fusion.4), kind=kCustom, calls=%fused_computation.clone.1.clone | custom fusion | bytes 2105344 | tf_op jit(solution)/shard_map/while/body/eval_jaxpr/gather | solution.py:40
  111.7 5.5 %gather_fusion.1 = f32[2048,128]{1,0:T(8,128)S(1)} fusion(f32[2048,128]{1,0:T(8,128)S(1)} %copy-done, s32[2048]{0:T(1024)S(1)} %broadcast_clamp_fusion.4), kind=kCustom, calls=%fused_computation.1.clone.1.clone | custom fusion | bytes 2105344 | tf_op jit(solution)/shard_map/while/body/eval_jaxpr/gather | solution.py:40
  118.1 1.5 dynamic_update_slice.31
  120.0 6.7 %gather_fusion = f32[2048,128]{1,0:T(8,128)S(1)} fusion(f32[2048,128]{1,0:T(8,128)} %get-tuple-element.438, s32[2048]{0:T(1024)S(1)} %broadcast_clamp_fusion.4), kind=kCustom, calls=%fused_computation.clone.1.clone | custom fusion | bytes 2105344 | tf_op jit(solution)/shard_map/while/body/eval_jaxpr/gather | solution.py:40
  127.0 0.9 copy-done
  128.0 5.5 %gather_fusion.1 = f32[2048,128]{1,0:T(8,128)S(1)} fusion(f32[2048,128]{1,0:T(8,128)S(1)} %copy-done, s32[2048]{0:T(1024)S(1)} %broadcast_clamp_fusion.4), kind=kCustom, calls=%fused_computation.1.clone.1.clone | custom fusion | bytes 2105344 | tf_op jit(solution)/shard_map/while/body/eval_jaxpr/gather | solution.py:40
  134.4 1.5 dynamic_update_slice.31
  136.3 6.7 %gather_fusion = f32[2048,128]{1,0:T(8,128)S(1)} fusion(f32[2048,128]{1,0:T(8,128)} %get-tuple-element.438, s32[2048]{0:T(1024)S(1)} %broadcast_clamp_fusion.4), kind=kCustom, calls=%fused_computation.clone.1.clone | custom fusion | bytes 2105344 | tf_op jit(solution)/shard_map/while/body/eval_jaxpr/gather | solution.py:40
  143.3 0.9 copy-done
  144.2 5.5 %gather_fusion.1 = f32[2048,128]{1,0:T(8,128)S(1)} fusion(f32[2048,128]{1,0:T(8,128)S(1)} %copy-done, s32[2048]{0:T(1024)S(1)} %broadcast_clamp_fusion.4), kind=kCustom, calls=%fused_computation.1.clone.1.clone | custom fusion | bytes 2105344 | tf_op jit(solution)/shard_map/while/body/eval_jaxpr/gather | solution.py:40
  150.7 1.5 dynamic_update_slice.31
  152.5 6.7 %gather_fusion = f32[2048,128]{1,0:T(8,128)S(1)} fusion(f32[2048,128]{1,0:T(8,128)} %get-tuple-element.438, s32[2048]{0:T(1024)S(1)} %broadcast_clamp_fusion.4), kind=kCustom, calls=%fused_computation.clone.1.clone | custom fusion | bytes 2105344 | tf_op jit(solution)/shard_map/while/body/eval_jaxpr/gather | solution.py:40
  160.4 5.5 %gather_fusion.1 = f32[2048,128]{1,0:T(8,128)S(1)} fusion(f32[2048,128]{1,0:T(8,128)S(1)} %copy-done, s32[2048]{0:T(1024)S(1)} %broadcast_clamp_fusion.4), kind=kCustom, calls=%fused_computation.1.clone.1.clone | custom fusion | bytes 2105344 | tf_op jit(solution)/shard_map/while/body/eval_jaxpr/gather | solution.py:40
  166.9 1.5 dynamic_update_slice.31
  168.7 6.7 %gather_fusion = f32[2048,128]{1,0:T(8,128)S(1)} fusion(f32[2048,128]{1,0:T(8,128)} %get-tuple-element.438, s32[2048]{0:T(1024)S(1)} %broadcast_clamp_fusion.4), kind=kCustom, calls=%fused_computation.clone.1.clone | custom fusion | bytes 2105344 | tf_op jit(solution)/shard_map/while/body/eval_jaxpr/gather | solution.py:40
  176.7 5.5 %gather_fusion.1 = f32[2048,128]{1,0:T(8,128)S(1)} fusion(f32[2048,128]{1,0:T(8,128)S(1)} %copy-done, s32[2048]{0:T(1024)S(1)} %broadcast_clamp_fusion.4), kind=kCustom, calls=%fused_computation.1.clone.1.clone | custom fusion | bytes 2105344 | tf_op jit(solution)/shard_map/while/body/eval_jaxpr/gather | solution.py:40
  183.1 1.5 dynamic_update_slice.31
  185.0 6.7 %gather_fusion = f32[2048,128]{1,0:T(8,128)S(1)} fusion(f32[2048,128]{1,0:T(8,128)} %get-tuple-element.438, s32[2048]{0:T(1024)S(1)} %broadcast_clamp_fusion.4), kind=kCustom, calls=%fused_computation.clone.1.clone | custom fusion | bytes 2105344 | tf_op jit(solution)/shard_map/while/body/eval_jaxpr/gather | solution.py:40
  192.9 5.5 %gather_fusion.1 = f32[2048,128]{1,0:T(8,128)S(1)} fusion(f32[2048,128]{1,0:T(8,128)S(1)} %copy-done, s32[2048]{0:T(1024)S(1)} %broadcast_clamp_fusion.4), kind=kCustom, calls=%fused_computation.1.clone.1.clone | custom fusion | bytes 2105344 | tf_op jit(solution)/shard_map/while/body/eval_jaxpr/gather | solution.py:40
  199.4 1.5 dynamic_update_slice.31
  201.0 1.5 all_to_all.20
  202.6 3.3 all-to-all-start.1
  206.6 6.1 %all-to-all-done.1 = f32[8,1,2048]{2,1,0:T(1,128)S(1)} async-done(((f32[8,1,2048]{2,1,0:T(1,128)}), f32[8,1,2048]{2,1,0:T(1,128)S(1)}, u32[]{:S(2)}, u32[]{:S(2)}) %all-to-all-start.1) | async-done | bytes 65568 | tf_op jit(solution)/shard_map/all_to_all | solution.py:135
  212.8 3.3 all-to-all-start.2
  216.1 45.5 %gather_fusion.3 = f32[8192]{0:T(1024)S(1)} fusion(f32[16384]{0:T(1024)S(1)} %bitcast.159, s32[8192]{0:T(1024)S(1)} %broadcast_clamp_fusion.1), kind=kCustom, calls=%fused_computation.3 | custom fusion | bytes 98304 | tf_op jit(solution)/shard_map/gather | solution.py:137
  262.0 45.5 %gather_fusion.5 = f32[8192]{0:T(1024)S(1)} fusion(f32[16384]{0:T(1024)S(1)} %bitcast.160, s32[8192]{0:T(1024)S(1)} %broadcast_clamp_fusion.1), kind=kCustom, calls=%fused_computation.5 | custom fusion | bytes 98304 | tf_op jit(solution)/shard_map/gather | solution.py:136
  308.6 4.4 %gather_fusion.2 = f32[1024,128]{1,0:T(8,128)S(1)} fusion(f32[4096,128]{1,0:T(8,128)} %all-gather.7.cloned.1.call-done, s32[1024]{0:T(1024)S(1)} %get-tuple-element.260), kind=kCustom, calls=%fused_computation.2 | custom fusion | bytes 1052672 | tf_op jit(solution)/shard_map/while/body/eval_jaxpr/gather | solution.py:40
  313.2 4.4 %gather_fusion.4 = f32[1024,128]{1,0:T(8,128)S(1)} fusion(f32[4096,128]{1,0:T(8,128)} %all-gather.13.cloned.1.call-done, s32[1024]{0:T(1024)S(1)} %get-tuple-element.260), kind=kCustom, calls=%fused_computation.4 | custom fusion | bytes 1052672 | tf_op jit(solution)/shard_map/while/body/eval_jaxpr/gather | solution.py:40
  318.2 5.2 %all-gather = f32[4096]{0:T(1024)S(1)} all-gather(f32[1024]{0:T(1024)S(1)} %get-tuple-element.258), channel_id=2, replica_groups=mesh['morton'=8,'level'=4] {'level'}, dimensions={0}, use_global_device_ids=true | all-gather | bytes 20480 | tf_op jit(solution)/shard_map/all_gather | solution.py:146
  323.5 5.2 %all-gather.1 = f32[4096]{0:T(1024)S(1)} all-gather(f32[1024]{0:T(1024)S(1)} %get-tuple-element.257), channel_id=3, replica_groups=mesh['morton'=8,'level'=4] {'level'}, dimensions={0}, use_global_device_ids=true | all-gather | bytes 20480 | tf_op jit(solution)/shard_map/all_gather | solution.py:145
  (209 shorter events, 27.9 us)
Async XLA Ops:
  7.2 17.3 %copy-start.1 = (s32[8192,1]{0,1:T(1,128)S(1)}, s32[8192,1]{0,1:T(1,128)}, u32[]{:S(2)}) copy-start(s32[8192,1]{0,1:T(1,128)} %param.25) | copy-start | bytes 98308
  7.2 17.3 %copy-start.6 = (s32[8192]{0:T(1024)S(1)}, s32[8192]{0:T(1024)}, u32[]{:S(2)}) copy-start(s32[8192]{0:T(1024)} %param.26) | copy-start | bytes 98308
  7.2 17.3 %copy-start.5 = (s32[8192]{0:T(1024)S(1)}, s32[8192]{0:T(1024)}, u32[]{:S(2)}) copy-start(s32[8192]{0:T(1024)} %param.27) | copy-start | bytes 98308
  7.2 17.3 %copy-start.4 = (s32[8192]{0:T(1024)S(1)}, s32[8192]{0:T(1024)}, u32[]{:S(2)}) copy-start(s32[8192]{0:T(1024)} %param.28) | copy-start | bytes 98308
  7.2 17.3 %copy-start.3 = (s32[8192]{0:T(1024)S(1)}, s32[8192]{0:T(1024)}, u32[]{:S(2)}) copy-start(s32[8192]{0:T(1024)} %param.29) | copy-start | bytes 98308
  7.2 63.8 %all-gather.11.cloned.1.call-start = ((), (), s32[]{:S(2)}) async-start(), calls=%async_computation.5 | async-start | bytes 1310720 | tf_op jit(solution)/shard_map/all_gather | solution.py:116
  8.0 63.1 %all-gather.9.cloned.1.call-start = ((), (), s32[]{:S(2)}) async-start(), calls=%async_computation.4 | async-start | bytes 1310720 | tf_op jit(solution)/shard_map/all_gather | solution.py:115
  8.7 55.0 %copy-start.2 = (s32[1024]{0:T(1024)S(1)}, s32[1024]{0:T(1024)}, u32[]{:S(2)}) copy-start(s32[1024]{0:T(1024)} %param.23) | copy-start | bytes 12292
  8.7 55.0 %copy-start.7 = (s32[1024]{0:T(1024)S(1)}, s32[1024]{0:T(1024)}, u32[]{:S(2)}) copy-start(s32[1024]{0:T(1024)} %param.24) | copy-start | bytes 12292
  8.7 299.9 %all-gather.7.cloned.1.call-start = ((), (), s32[]{:S(2)}) async-start(), calls=%async_computation.3 | async-start | bytes 2359296 | tf_op jit(solution)/shard_map/all_gather | solution.py:111
  55.8 14.9 %all-to-all-start = ((s32[8,1,2048]{2,1,0:T(1,128)}), s32[8,1,2048]{2,1,0:T(1,128)S(1)}, u32[]{:S(2)}, u32[]{:S(2)}) async-start(s32[8,1,2048]{2,1,0:T(1,128)} %bitcast.16), calls=%async_computation | async-start | bytes 131072 | tf_op jit(solution)/shard_map/all_to_all | solution.py:132
  63.1 250.1 %all-gather.13.cloned.1.call-start = ((), (), s32[]{:S(2)}) async-start(), calls=%async_computation.6 | async-start | bytes 2359296 | tf_op jit(solution)/shard_map/all_gather | solution.py:112
  71.1 134.8 %copy-start.8 = (s32[1024]{0:T(1024)S(1)}, s32[1024]{0:T(1024)}, u32[]{:S(2)}) copy-start(s32[1024]{0:T(1024)} %param.22) | copy-start | bytes 12292
  71.1 134.8 %copy-start.9 = (s32[1024]{0:T(1024)S(1)}, s32[1024]{0:T(1024)}, u32[]{:S(2)}) copy-start(s32[1024]{0:T(1024)} %param.21) | copy-start | bytes 12292
  78.0 1.2 copy-start
  94.2 1.2 copy-start
  110.4 1.2 copy-start
  126.7 1.3 copy-start
  143.0 1.2 copy-start
  159.2 1.2 copy-start
  175.4 1.2 copy-start
  191.7 1.2 copy-start
  202.6 10.2 %all-to-all-start.1 = ((f32[8,1,2048]{2,1,0:T(1,128)}), f32[8,1,2048]{2,1,0:T(1,128)S(1)}, u32[]{:S(2)}, u32[]{:S(2)}) async-start(f32[8,1,2048]{2,1,0:T(1,128)} %all_to_all.20), calls=%async_computation.1 | async-start | bytes 131072 | tf_op jit(solution)/shard_map/all_to_all | solution.py:135
  212.8 49.2 %all-to-all-start.2 = ((f32[8,1,2048]{2,1,0:T(1,128)}), f32[8,1,2048]{2,1,0:T(1,128)S(1)}, u32[]{:S(2)}, u32[]{:S(2)}) async-start(f32[8,1,2048]{2,1,0:T(1,128)} %all_to_all.22), calls=%async_computation.2 | async-start | bytes 131072 | tf_op jit(solution)/shard_map/all_to_all | solution.py:134
Sparse Core Ops, SparseCore 0:
  9.6 19.4 all-gather.10
  30.6 16.6 all-gather.8
  49.5 50.1 all-gather.6
  101.7 47.6 all-gather.12
where the time goes:
time: 338 us; the launch traced here: 336 us
  local copies, waits for them, and re-layouts  259 us (77%)
  other arithmetic  21.5 us (6%)
  waiting for transfers between devices  15.8 us (5%)
  between operations  14.2 us (4%)
  starting transfers between devices  14.1 us (4%)
  blocking collectives  10.4 us (3%)
    gather x18, local copies, waits for them, and re-layouts, sample_one_block(): dens_table[row_index]  60.7 us
    gather x18, local copies, waits for them, and re-layouts, sample_one_block(): emis_table[row_index]  50.9 us
    gather x1, local copies, waits for them, and re-layouts, shards(): seg_depth = depths_back.reshape(-1)[destination].reshape(pixels, -1)  45.5 us
    gather x1, local copies, waits for them, and re-layouts, shards(): seg_color = colors_back.reshape(-1)[destination].reshape(pixels, -1)  45.5 us
    scatter x1, local copies, waits for them, and re-layouts, shards(): jnp.zeros((n_morton * capacity,), jnp.int32).at[destination].set(codes)  31 us
    dynamic_update_slice x16, local copies, waits for them, and re-layouts, sample_table(): colors, depths = lax.map(sample_one_block, shaped)  13.2 us
    another operation x10, other arithmetic  9.8 us
    all_to_all x1, starting transfers between devices, shards(): lax.all_to_all(requests, 'morton', split_axis=0, concat_axis=0, tiled=True)  7.28 us
  transfers between devices with their start and end apart: 7, of which 2 were waited for; matrix products, arithmetic and copies ran while one was open for 79% of the time, Pallas kernels for 0%

commit v1 on v0

v1 whole, which is shorter than its diff:
```python
import functools

import jax
import jax.numpy as jnp
from jax import lax
from jax.experimental import pallas as pl
from jax.experimental.pallas import tpu as pltpu
from jax.sharding import PartitionSpec as P

BRICK = 32
PER_ROW = 128 // BRICK
AXES = ("morton", "level")
F32 = jnp.float32
BF16 = jnp.bfloat16


def split3(x):
    hi = x.astype(BF16)
    rest = x - hi.astype(F32)
    mid = rest.astype(BF16)
    lo = (rest - mid.astype(F32)).astype(BF16)
    return hi, mid, lo


def split2(x):
    hi = x.astype(BF16)
    return hi, (x - hi.astype(F32)).astype(BF16)


def flag(cond):
    return jnp.where(cond, F32(1.0), F32(0.0)).astype(BF16)


def iota(shape, axis):
    return lax.broadcasted_iota(jnp.int32, shape, axis)


def line(ref, start, rows):
    return jnp.concatenate([ref[start + j : start + j + 1, :] for j in range(rows)], axis=1)


def nt_dot(a, b):
    return lax.dot_general(a, b, (((1,), (1,)), ((), ())), preferred_element_type=F32)


def route_kernel(owner, brick, lane, entry, count, cbrick, clane, centry, ccount, msg, ranks, *, n_dev, n_level, cap, quarter):
    rows = owner.shape[0]
    per = 4
    width = per * 128
    upper = flag(iota((width, width), 0) < iota((width, width), 1))
    t_ids = iota((n_dev, width), 0)
    r_ids = iota((cap, width), 0)
    offsets = jnp.zeros((n_dev, 1), F32)
    acc = jnp.zeros((3 * n_dev, cap), F32)
    for c in range(rows // per):
        own = line(owner, c * per, per)
        hit = own == t_ids
        hot = jnp.where(hit, F32(1.0), F32(0.0))
        before = jnp.dot(hot.astype(BF16), upper, preferred_element_type=F32)
        rank = jnp.sum(hot * (before + offsets), axis=0, keepdims=True)
        offsets = offsets + before[:, width - 1 :] + hot[:, width - 1 :]
        rank_int = rank.astype(jnp.int32)
        ranks[c : c + 1, :] = rank_int
        cell = line(brick, c * per, per) * (BRICK * BRICK) + line(lane, c * per, per)
        code = (cell * BRICK + line(entry, c * per, per)) * 64 + line(count, c * per, per)
        parts = [(code & 255), ((code >> 8) & 255), (code >> 16)]
        left = jnp.concatenate(
            [jnp.where(hit, part.astype(F32), F32(0.0)).astype(BF16) for part in parts], axis=0
        )
        acc = acc + nt_dot(left, flag(rank_int == r_ids))
    fine = acc[:n_dev] + acc[n_dev : 2 * n_dev] * F32(256.0) + acc[2 * n_dev :] * F32(65536.0)
    msg[:, quarter:] = fine.astype(jnp.int32)
    level_of = iota((n_dev, quarter), 0) % n_level
    crows = quarter // 128
    out = jnp.zeros((n_dev, quarter), jnp.int32)
    for q in range(n_level):
        cell = line(cbrick, q * crows, crows) * (BRICK * BRICK) + line(clane, q * crows, crows)
        code = (cell * BRICK + line(centry, q * crows, crows)) * 64 + line(ccount, q * crows, crows)
        out = jnp.where(level_of == q, code, out)
    msg[:, :quarter] = out


def march_block(table, code, base):
    rows = table.shape[2]
    width = code.shape[1]
    row = (code >> 13) - base
    hot = flag(row == iota((rows, width), 0))
    both = jnp.dot(table[0], hot, preferred_element_type=F32) + jnp.dot(
        table[1], hot, preferred_element_type=F32
    )
    which = (code >> 11) & (PER_ROW - 1)
    entry = (code >> 6) & (BRICK - 1)
    end = entry + (code & 63)

    def pick(start):
        out = both[start : start + BRICK]
        for j in range(1, PER_ROW):
            out = jnp.where(which == j, both[start + j * BRICK : start + (j + 1) * BRICK], out)
        return out

    dens, emis = pick(0), pick(128)
    step = iota((BRICK, width), 0)
    optical = jnp.where((step >= entry) & (step < end), dens, F32(0.0))
    run = jnp.zeros((1, width), F32)
    color = jnp.zeros((8, width), F32)
    sub = iota((8, width), 0)
    for g in range(BRICK // 8):
        mine = optical[g * 8 : g * 8 + 8]
        scan = mine
        for shift in (1, 2, 4):
            scan = scan + jnp.where(sub >= shift, pltpu.roll(scan, shift, 0), F32(0.0))
        before = (scan - mine) + run
        color = color + jnp.exp(-before) * (1.0 - jnp.exp(-mine)) * emis[g * 8 : g * 8 + 8]
        run = run + scan[7:8]
    return jnp.sum(color, axis=0, keepdims=True), run


def load_table(dens, emis, table):
    dens_hi, dens_lo = split2(dens[...].T)
    emis_hi, emis_lo = split2(emis[...].T)
    table[0, :128, :] = dens_hi
    table[0, 128:, :] = emis_hi
    table[1, :128, :] = dens_lo
    table[1, 128:, :] = emis_lo


def march_kernel(base, msg, fdens, femis, cdens, cemis, out, ftable, ctable, *, quarter):
    n_dev = msg.shape[0]
    load_table(fdens, femis, ftable)
    load_table(cdens, cemis, ctable)
    start = base[0]

    def body(s, carry):
        code = msg[pl.ds(s, 1), :]
        near = march_block(ctable, code[:, :quarter], start)
        far = march_block(ftable, code[:, quarter:], 0)
        out[pl.ds(s, 1), :] = jnp.concatenate([near[0], far[0], near[1], far[1]], axis=1)
        return carry

    lax.fori_loop(0, n_dev, body, 0)


def blend_kernel(back, owner, ranks, out, color_ref, depth_ref, *, n_level, quarter, per_pixel):
    n_dev, width = back.shape[0], back.shape[1] // 2
    cap = width - quarter
    rows = owner.shape[0]
    per = 4
    chunk = per * 128
    line_len = quarter * per_pixel
    stacked = jnp.concatenate(split3(back[:, quarter:width]) + split3(back[:, width + quarter :]), axis=0)
    t_ids = iota((n_dev, chunk), 0)
    r_ids = iota((cap, chunk), 0)
    for c in range(rows // per):
        hit = line(owner, c * per, per) == t_ids
        hot = flag(ranks[c : c + 1, :] == r_ids)
        got = jnp.dot(stacked, hot, preferred_element_type=F32)
        picked = [
            jnp.sum(
                jnp.where(
                    hit,
                    got[k * n_dev : (k + 1) * n_dev]
                    + got[(k + 1) * n_dev : (k + 2) * n_dev]
                    + got[(k + 2) * n_dev : (k + 3) * n_dev],
                    F32(0.0),
                ),
                axis=0,
                keepdims=True,
            )
            for k in (0, 3)
        ]
        at, off = divmod(c * chunk, line_len)
        color_ref[at : at + 1, off : off + chunk] = picked[0]
        depth_ref[at : at + 1, off : off + chunk] = picked[1]
    depth = depth_ref[...]
    slot = iota((n_level, line_len), 1) % per_pixel
    scan = depth
    shift = 1
    while shift < per_pixel:
        scan = scan + jnp.where(slot >= shift, pltpu.roll(scan, shift, 1), F32(0.0))
        shift *= 2
    seen = jnp.exp(-(scan - depth)) * color_ref[...]
    gather = flag(iota((line_len, quarter), 0) // per_pixel == iota((line_len, quarter), 1))
    sums = jnp.dot(
        jnp.concatenate([x.astype(F32) for x in split3(seen) + split3(depth)], axis=0).astype(BF16),
        gather,
        preferred_element_type=F32,
    )
    part = [sums[k * n_level : (k + 1) * n_level] for k in range(6)]
    fine_color, fine_depth = part[0] + part[1] + part[2], part[3] + part[4] + part[5]

    def coarse(start):
        block = back[:, start : start + quarter]
        total = block[:n_level]
        for m in range(1, n_dev // n_level):
            total = total + block[m * n_level : (m + 1) * n_level]
        return total

    coarse_color, coarse_depth = coarse(0), coarse(width)
    out[:, :quarter] = coarse_color + jnp.exp(-coarse_depth) * fine_color
    out[:, quarter:] = coarse_depth + fine_depth


def shards(
    coarse_density,
    coarse_emission,
    fine_density,
    fine_emission,
    coarse_brick,
    coarse_lane,
    coarse_entry,
    coarse_count,
    fine_owner,
    fine_brick,
    fine_lane,
    fine_entry,
    fine_count,
):
    n_morton = lax.axis_size("morton")
    n_level = lax.axis_size("level")
    n_dev = n_morton * n_level
    segments = fine_brick.shape[0]
    pixels = coarse_brick.shape[0]
    quarter = pixels // n_level
    cap = -(-(2 * segments // n_dev) // 128) * 128
    width = quarter + cap
    owner = fine_owner.reshape(-1, 128)
    fine = [x.reshape(-1, 128) for x in (fine_brick, fine_lane, fine_entry, fine_count)]
    coarse = [x.reshape(-1, 128) for x in (coarse_brick, coarse_lane, coarse_entry, coarse_count)]
    msg, ranks = pl.pallas_call(
        functools.partial(route_kernel, n_dev=n_dev, n_level=n_level, cap=cap, quarter=quarter),
        out_shape=(
            jax.ShapeDtypeStruct((n_dev, width), jnp.int32),
            jax.ShapeDtypeStruct((segments // 512, 512), jnp.int32),
        ),
        name="route",
    )(owner, *fine, *coarse)
    msg = lax.all_to_all(msg, AXES, split_axis=0, concat_axis=0, tiled=True)
    base = (lax.axis_index("morton") * coarse_density.shape[0]).reshape(1)
    vmem = pl.BlockSpec(memory_space=pltpu.VMEM)
    served = pl.pallas_call(
        functools.partial(march_kernel, quarter=quarter),
        out_shape=jax.ShapeDtypeStruct((n_dev, 2 * width), F32),
        in_specs=[pl.BlockSpec(memory_space=pltpu.SMEM)] + [vmem] * 5,
        out_specs=vmem,
        scratch_shapes=[
            pltpu.VMEM((2, 256, fine_density.shape[0]), BF16),
            pltpu.VMEM((2, 256, coarse_density.shape[0]), BF16),
        ],
        name="march",
    )(base, msg, fine_density, fine_emission, coarse_density, coarse_emission)
    back = lax.all_to_all(served, AXES, split_axis=0, concat_axis=0, tiled=True)
    per_pixel = segments // pixels
    slab = pl.pallas_call(
        functools.partial(blend_kernel, n_level=n_level, quarter=quarter, per_pixel=per_pixel),
        out_shape=jax.ShapeDtypeStruct((n_level, 2 * quarter), F32),
        scratch_shapes=[pltpu.VMEM((n_level, quarter * per_pixel), F32)] * 2,
        name="blend",
    )(back, owner, ranks)
    slabs = lax.all_to_all(slab, "level", split_axis=0, concat_axis=0, tiled=True)
    part_color, part_depth = slabs[:, :quarter], slabs[:, quarter:]
    in_front = jnp.cumsum(part_depth, axis=0) - part_depth
    image_color = jnp.sum(jnp.exp(-in_front) * part_color, axis=0)
    transmittance = jnp.exp(-jnp.sum(part_depth, axis=0))
    return (image_color, transmittance)


def solution(mesh):
    split = P(AXES)
    rows = P(AXES, None)
    return jax.shard_map(
        shards,
        mesh=mesh,
        in_specs=(P("morton", None), P("morton", None), rows, rows)
        + (split,) * 4
        + (rows,)
        + (split,) * 4,
        out_specs=(split, split),
        check_vma=False,
    )
```

time: 338 us -> 74.5 us (0.22)
  local copies, waits for them, and re-layouts: 259 us -> 4.79 us
  Pallas kernels: 0 us -> 35.5 us
  other arithmetic: 21.5 us -> 1.2 us
  between operations: 14.2 us -> 0.66 us
  waiting for transfers between devices: 15.8 us -> 7.78 us
  starting transfers between devices: 14.1 us -> 7.32 us
  blocking collectives: 10.4 us -> 16.8 us
    gather x38 -> x0, local copies, waits for them, and re-layouts: 203 us -> none  [the longest x18 60.7 us: sample_one_block(): dens_table[row_index]]
    pallas_call x0 -> x3, Pallas kernels: none -> 35.5 us  [the longest x1 24.1 us: shards(): pl.pallas_call(functools.partial(march_kernel, quarter=quarter), out_shap...]
    scatter x1 -> x0, local copies, waits for them, and re-layouts: 31 us -> none  [shards(): jnp.zeros((n_morton * capacity,), jnp.int32).at[destination].set(codes)]
    all_to_all x0 -> x2, blocking collectives: none -> 16.8 us  [the longest x1 10.7 us: shards(): back = lax.all_to_all(served, AXES, split_axis=0, concat_axis=0, tiled=True)]
    dynamic_update_slice x20 -> x0, local copies, waits for them, and re-layouts: 13.8 us -> none  [the longest x16 13.2 us: sample_table(): colors, depths = lax.map(sample_one_block, shaped)]
    another operation x20 -> x0, other arithmetic: 12.2 us -> none
    all_gather x2 -> x0, blocking collectives: 10.4 us -> none  [the longest x1 5.21 us: shards(): lax.all_gather(slab_depth.reshape(1, pixels), 'level', axis=0, tiled=True)]
    while x16 -> x0, local copies, waits for them, and re-layouts: 7.11 us -> none
  transfers between devices with their start and end apart: 7 -> 1, of which waited for: 2 -> 1; matrix products, arithmetic and copies ran while one was open for 79% -> 0% of each run, Pallas kernels for 0% -> 0%
where the time goes in v1:
time: 74.5 us; the launch traced here: 74.1 us
  Pallas kernels  35.5 us (48%)
  blocking collectives  16.8 us (23%)
  waiting for transfers between devices  7.78 us (10%)
  starting transfers between devices  7.32 us (10%)
  local copies, waits for them, and re-layouts  4.79 us (6%)
  other arithmetic  1.2 us (2%)
    pallas_call x1, Pallas kernels, shards(): pl.pallas_call(functools.partial(march_kernel, quarter=quarter), out_shap...  24.1 us
    all_to_all x1, blocking collectives, shards(): back = lax.all_to_all(served, AXES, split_axis=0, concat_axis=0, tiled=True)  10.7 us
    all_to_all x1, waiting for transfers between devices, shards(): msg = lax.all_to_all(msg, AXES, split_axis=0, concat_axis=0, tiled=True)  7.78 us
    all_to_all x1, starting transfers between devices, shards(): msg = lax.all_to_all(msg, AXES, split_axis=0, concat_axis=0, tiled=True)  7.32 us
    pallas_call x1, Pallas kernels, shards(): pl.pallas_call(functools.partial(route_kernel, n_dev=n_dev, n_level=n_lev...  6.94 us
    all_to_all x1, blocking collectives, shards(): lax.all_to_all(slab, 'level', split_axis=0, concat_axis=0, tiled=True)  6.15 us
    pallas_call x1, Pallas kernels, shards(): pl.pallas_call(functools.partial(blend_kernel, n_level=n_level, quarter=q...  4.55 us
    all_to_all x1, local copies, waits for them, and re-layouts, shards(): msg = lax.all_to_all(msg, AXES, split_axis=0, concat_axis=0, tiled=True)  1.63 us
  transfers between devices with their start and end apart: 1, of which 1 were waited for; matrix products, arithmetic and copies ran while one was open for 0% of the time, Pallas kernels for 0%

profile of v1, /device:TPU:0, one launch (start us, length us, event | category | flops | bytes accessed | tf_op | source)
XLA Modules:
  0.0 74.1 jit_solution(4916207519603724803)
XLA Ops:
  0.6 6.9 %route.1 = (s32[32,768]{1,0:T(8,128)}, s32[16,512]{1,0:T(8,128)}) custom-call(s32[64,128]{1,0:T(8,128)} %bitcast.25, s32[64,128]{1,0:T(8,128)} %bitcast.31, s32[64,128]{1,0:T(8,128)} %bitcast.32, s32[64,128]{1,0:T(8,128)} %bitcast.33, s32[64,128]{1,0:T(8,128)} %bitcast.34, s32[8,128]{1,0:T(8,128)} %bitcast.35, s32[8,128]{1,0:T(8,128)} %bitcast.36, ...), custom_call_target="tpu_custom_call" | custom-call | tf_op jit(solution)/shard_map/route/pallas_call | solution.py:229
  7.6 1.6 %copy.15 = s32[32,1,768]{2,1,0:T(1,128)} copy(s32[32,1,768]{2,0,1:T(8,128)} %bitcast.27) | data formatting | bytes 196608 | tf_op jit(solution)/shard_map/all_to_all | solution.py:237
  9.2 7.3 %all-to-all-start = ((s32[32,1,768]{2,1,0:T(1,128)}), s32[32,1,768]{2,1,0:T(1,128)S(1)}, u32[]{:S(2)}, u32[]{:S(2)}) async-start(s32[32,1,768]{2,1,0:T(1,128)} %copy.15), calls=%async_computation | async-start | bytes 196608 | tf_op jit(solution)/shard_map/all_to_all | solution.py:237
  16.5 7.8 %all-to-all-done = s32[32,1,768]{2,1,0:T(1,128)S(1)} async-done(((s32[32,1,768]{2,1,0:T(1,128)}), s32[32,1,768]{2,1,0:T(1,128)S(1)}, u32[]{:S(2)}, u32[]{:S(2)}) %all-to-all-start) | async-done | bytes 98336 | tf_op jit(solution)/shard_map/all_to_all | solution.py:237
  24.3 0.6 copy.25
  25.0 24.1 %march.1 = f32[32,1536]{1,0:T(8,128)} custom-call(s32[1]{0:T(128)} %bitcast.base, s32[32,768]{1,0:T(8,128)} %bitcast.24, f32[512,128]{1,0:T(8,128)} %fdens.1, f32[512,128]{1,0:T(8,128)} %femis.1, f32[512,128]{1,0:T(8,128)} %cdens.1, f32[512,128]{1,0:T(8,128)} %cemis.1), custom_call_target="tpu_custom_call" | custom-call | tf_op jit(solution)/shard_map/march/pallas_call | solution.py:240
  49.0 1.1 %copy.16 = f32[32,1,1536]{2,1,0:T(1,128)S(1)} copy(f32[32,1,1536]{2,0,1:T(8,128)} %bitcast.22) | data formatting | bytes 393216 | tf_op jit(solution)/shard_map/all_to_all | solution.py:251
  50.1 10.7 %all_to_all.34 = f32[32,1,1536]{2,1,0:T(1,128)S(1)} all-to-all(f32[32,1,1536]{2,1,0:T(1,128)S(1)} %copy.16), channel_id=1, replica_groups=mesh['morton'=8,'level'=4] {'morton','level'}, dimensions={0} | all-to-all | bytes 393216 | tf_op jit(solution)/shard_map/all_to_all | solution.py:251
  60.8 0.7 copy.24
  61.5 4.5 %blend.1 = f32[4,512]{1,0:T(4,128)} custom-call(f32[32,1536]{1,0:T(8,128)} %bitcast.23, s32[64,128]{1,0:T(8,128)} %bitcast.26, s32[16,512]{1,0:T(8,128)} %get-tuple-element.5.ranks), custom_call_target="tpu_custom_call" | custom-call | tf_op jit(solution)/shard_map/blend/pallas_call | solution.py:253
  66.0 0.7 copy.17
  66.7 6.2 %all_to_all.35 = f32[4,1,512]{2,1,0:T(1,128)S(1)} all-to-all(f32[4,1,512]{2,1,0:T(1,128)S(1)} %copy.17), channel_id=1, replica_groups=mesh['morton'=8,'level'=4] {'level'}, dimensions={0} | all-to-all | bytes 16384 | tf_op jit(solution)/shard_map/all_to_all | solution.py:259
  72.9 0.6 slice_reduce_fusion
  73.5 0.6 negate_exponential_fusion
  (3 shorter events, 0.0 us)
Async XLA Ops:
  9.2 15.1 %all-to-all-start = ((s32[32,1,768]{2,1,0:T(1,128)}), s32[32,1,768]{2,1,0:T(1,128)S(1)}, u32[]{:S(2)}, u32[]{:S(2)}) async-start(s32[32,1,768]{2,1,0:T(1,128)} %copy.15), calls=%async_computation | async-start | bytes 196608 | tf_op jit(solution)/shard_map/all_to_all | solution.py:237

commit v2 on v1

--- a/solution.py
+++ b/solution.py
@@ -9,6 +9,7 @@
 
 BRICK = 32
 PER_ROW = 128 // BRICK
+UNROLL = 8
 AXES = ("morton", "level")
 F32 = jnp.float32
 BF16 = jnp.bfloat16
@@ -69,7 +70,7 @@
         )
         acc = acc + nt_dot(left, flag(rank_int == r_ids))
     fine = acc[:n_dev] + acc[n_dev : 2 * n_dev] * F32(256.0) + acc[2 * n_dev :] * F32(65536.0)
-    msg[:, quarter:] = fine.astype(jnp.int32)
+    fine = fine.astype(jnp.int32)
     level_of = iota((n_dev, quarter), 0) % n_level
     crows = quarter // 128
     out = jnp.zeros((n_dev, quarter), jnp.int32)
@@ -77,17 +78,24 @@
         cell = line(cbrick, q * crows, crows) * (BRICK * BRICK) + line(clane, q * crows, crows)
         code = (cell * BRICK + line(centry, q * crows, crows)) * 64 + line(ccount, q * crows, crows)
         out = jnp.where(level_of == q, code, out)
-    msg[:, :quarter] = out
+    msg[:, 0, :quarter] = out
+    msg[:, 0, quarter:] = fine
 
 
 def march_block(table, code, base):
-    rows = table.shape[2]
+    rows = table.shape[1]
     width = code.shape[1]
     row = (code >> 13) - base
-    hot = flag(row == iota((rows, width), 0))
-    both = jnp.dot(table[0], hot, preferred_element_type=F32) + jnp.dot(
-        table[1], hot, preferred_element_type=F32
-    )
+    seg = min(rows, 256)
+    lane_row = iota((seg, width), 0).astype(F32).astype(BF16)
+    parts = []
+    for h in range(rows // seg):
+        mine = row - h * seg
+        mine = jnp.where((mine >= 0) & (mine < seg), mine, -1).astype(F32).astype(BF16)
+        parts.append(jnp.where(lane_row == mine, BF16(1.0), BF16(0.0)))
+    hot = jnp.concatenate(parts, axis=0)
+    pieces = jnp.dot(table[...], hot, preferred_element_type=F32)
+    both = pieces[:256] + pieces[256:]
     which = (code >> 11) & (PER_ROW - 1)
     entry = (code >> 6) & (BRICK - 1)
     end = entry + (code & 63)
@@ -118,10 +126,10 @@
 def load_table(dens, emis, table):
     dens_hi, dens_lo = split2(dens[...].T)
     emis_hi, emis_lo = split2(emis[...].T)
-    table[0, :128, :] = dens_hi
-    table[0, 128:, :] = emis_hi
-    table[1, :128, :] = dens_lo
-    table[1, 128:, :] = emis_lo
+    table[:128, :] = dens_hi
+    table[128:256, :] = emis_hi
+    table[256:384, :] = dens_lo
+    table[384:, :] = emis_lo
 
 
 def march_kernel(base, msg, fdens, femis, cdens, cemis, out, ftable, ctable, *, quarter):
@@ -131,23 +139,27 @@
     start = base[0]
 
     def body(s, carry):
-        code = msg[pl.ds(s, 1), :]
+        code = msg[s]
         near = march_block(ctable, code[:, :quarter], start)
         far = march_block(ftable, code[:, quarter:], 0)
-        out[pl.ds(s, 1), :] = jnp.concatenate([near[0], far[0], near[1], far[1]], axis=1)
+        out[s] = jnp.concatenate([near[0], far[0], near[1], far[1]], axis=1)
         return carry
 
-    lax.fori_loop(0, n_dev, body, 0)
+    lax.fori_loop(0, n_dev, body, 0, unroll=UNROLL)
 
 
 def blend_kernel(back, owner, ranks, out, color_ref, depth_ref, *, n_level, quarter, per_pixel):
-    n_dev, width = back.shape[0], back.shape[1] // 2
+    n_dev, width = back.shape[0], back.shape[2] // 2
+
+    def cut(start, end):
+        return back[:, 0, start:end]
+
     cap = width - quarter
     rows = owner.shape[0]
     per = 4
     chunk = per * 128
     line_len = quarter * per_pixel
-    stacked = jnp.concatenate(split3(back[:, quarter:width]) + split3(back[:, width + quarter :]), axis=0)
+    stacked = jnp.concatenate(split3(cut(quarter, width)) + split3(cut(width + quarter, 2 * width)), axis=0)
     t_ids = iota((n_dev, chunk), 0)
     r_ids = iota((cap, chunk), 0)
     for c in range(rows // per):
@@ -189,15 +201,27 @@
     fine_color, fine_depth = part[0] + part[1] + part[2], part[3] + part[4] + part[5]
 
     def coarse(start):
-        block = back[:, start : start + quarter]
+        block = cut(start, start + quarter)
         total = block[:n_level]
         for m in range(1, n_dev // n_level):
             total = total + block[m * n_level : (m + 1) * n_level]
         return total
 
     coarse_color, coarse_depth = coarse(0), coarse(width)
-    out[:, :quarter] = coarse_color + jnp.exp(-coarse_depth) * fine_color
-    out[:, quarter:] = coarse_depth + fine_depth
+    out[:, 0, :quarter] = coarse_color + jnp.exp(-coarse_depth) * fine_color
+    out[:, 0, quarter:] = coarse_depth + fine_depth
+
+
+def finish_kernel(slabs, color_ref, through_ref):
+    quarter = slabs.shape[2] // 2
+    color = jnp.zeros((1, quarter), F32)
+    depth = jnp.zeros((1, quarter), F32)
+    for s in range(slabs.shape[0]):
+        part = slabs[s]
+        color = color + jnp.exp(-depth) * part[:, :quarter]
+        depth = depth + part[:, quarter:]
+    color_ref[...] = color
+    through_ref[...] = jnp.exp(-depth)
 
 
 def shards(
@@ -229,39 +253,43 @@
     msg, ranks = pl.pallas_call(
         functools.partial(route_kernel, n_dev=n_dev, n_level=n_level, cap=cap, quarter=quarter),
         out_shape=(
-            jax.ShapeDtypeStruct((n_dev, width), jnp.int32),
+            pltpu.VMEM((n_dev, 1, width), jnp.int32),
             jax.ShapeDtypeStruct((segments // 512, 512), jnp.int32),
         ),
         name="route",
     )(owner, *fine, *coarse)
     msg = lax.all_to_all(msg, AXES, split_axis=0, concat_axis=0, tiled=True)
+    msg = pltpu.with_memory_space_constraint(msg, pltpu.VMEM)
     base = (lax.axis_index("morton") * coarse_density.shape[0]).reshape(1)
     vmem = pl.BlockSpec(memory_space=pltpu.VMEM)
     served = pl.pallas_call(
         functools.partial(march_kernel, quarter=quarter),
-        out_shape=jax.ShapeDtypeStruct((n_dev, 2 * width), F32),
+        out_shape=pltpu.VMEM((n_dev, 1, 2 * width), F32),
         in_specs=[pl.BlockSpec(memory_space=pltpu.SMEM)] + [vmem] * 5,
         out_specs=vmem,
         scratch_shapes=[
-            pltpu.VMEM((2, 256, fine_density.shape[0]), BF16),
-            pltpu.VMEM((2, 256, coarse_density.shape[0]), BF16),
+            pltpu.VMEM((512, fine_density.shape[0]), BF16),
+            pltpu.VMEM((512, coarse_density.shape[0]), BF16),
         ],
         name="march",
     )(base, msg, fine_density, fine_emission, coarse_density, coarse_emission)
     back = lax.all_to_all(served, AXES, split_axis=0, concat_axis=0, tiled=True)
+    back = pltpu.with_memory_space_constraint(back, pltpu.VMEM)
     per_pixel = segments // pixels
     slab = pl.pallas_call(
         functools.partial(blend_kernel, n_level=n_level, quarter=quarter, per_pixel=per_pixel),
-        out_shape=jax.ShapeDtypeStruct((n_level, 2 * quarter), F32),
+        out_shape=pltpu.VMEM((n_level, 1, 2 * quarter), F32),
         scratch_shapes=[pltpu.VMEM((n_level, quarter * per_pixel), F32)] * 2,
         name="blend",
     )(back, owner, ranks)
     slabs = lax.all_to_all(slab, "level", split_axis=0, concat_axis=0, tiled=True)
-    part_color, part_depth = slabs[:, :quarter], slabs[:, quarter:]
-    in_front = jnp.cumsum(part_depth, axis=0) - part_depth
-    image_color = jnp.sum(jnp.exp(-in_front) * part_color, axis=0)
-    transmittance = jnp.exp(-jnp.sum(part_depth, axis=0))
-    return (image_color, transmittance)
+    slabs = pltpu.with_memory_space_constraint(slabs, pltpu.VMEM)
+    image_color, transmittance = pl.pallas_call(
+        finish_kernel,
+        out_shape=(jax.ShapeDtypeStruct((1, quarter), F32),) * 2,
+        name="finish",
+    )(slabs)
+    return (image_color.reshape(quarter), transmittance.reshape(quarter))
 
 
 def solution(mesh):

time: 74.5 us -> 60.3 us (0.81)
  Pallas kernels: 35.5 us -> 27.4 us
  local copies, waits for them, and re-layouts: 4.79 us -> 0 us
  other arithmetic: 1.2 us -> 0 us
    pallas_call x1, Pallas kernels: 24.1 us -> 15.9 us  [shards(): pl.pallas_call(functools.partial(march_kernel, quarter=quarter), out_shap...]
    all_to_all x3 -> x0, local copies, waits for them, and re-layouts: 3.46 us -> none  [the longest x1 1.63 us: shards(): msg = lax.all_to_all(msg, AXES, split_axis=0, concat_axis=0, tiled=True)]
    unnamed x3 -> x0, local copies, waits for them, and re-layouts: 1.33 us -> none
where the time goes in v2:
time: 60.3 us; the launch traced here: 59.9 us
  Pallas kernels  27.4 us (45%)
  blocking collectives  16.8 us (28%)
  waiting for transfers between devices  7.78 us (13%)
  starting transfers between devices  7.32 us (12%)
  between operations  0.66 us (1%)
    pallas_call x1, Pallas kernels, shards(): pl.pallas_call(functools.partial(march_kernel, quarter=quarter), out_shap...  15.9 us
    all_to_all x1, blocking collectives, shards(): back = lax.all_to_all(served, AXES, split_axis=0, concat_axis=0, tiled=True)  10.7 us
    all_to_all x1, waiting for transfers between devices, shards(): msg = lax.all_to_all(msg, AXES, split_axis=0, concat_axis=0, tiled=True)  7.78 us
    all_to_all x1, starting transfers between devices, shards(): msg = lax.all_to_all(msg, AXES, split_axis=0, concat_axis=0, tiled=True)  7.32 us
    pallas_call x1, Pallas kernels, shards(): pl.pallas_call(functools.partial(route_kernel, n_dev=n_dev, n_level=n_lev...  6.96 us
    all_to_all x1, blocking collectives, shards(): lax.all_to_all(slab, 'level', split_axis=0, concat_axis=0, tiled=True)  6.15 us
    pallas_call x1, Pallas kernels, shards(): pl.pallas_call(functools.partial(blend_kernel, n_level=n_level, quarter=q...  3.89 us
  transfers between devices with their start and end apart: 1, of which 1 were waited for; matrix products, arithmetic and copies ran while one was open for 0% of the time, Pallas kernels for 0%

profile of v2, /device:TPU:0, one launch (start us, length us, event | category | flops | bytes accessed | tf_op | source)
XLA Modules:
  0.0 59.9 jit_solution(16389157724520781662)
XLA Ops:
  0.6 7.0 %route.1 = (s32[32,1,768]{2,1,0:T(1,128)}, s32[16,512]{1,0:T(8,128)}) custom-call(s32[64,128]{1,0:T(8,128)} %bitcast.12, s32[64,128]{1,0:T(8,128)} %bitcast.14, s32[64,128]{1,0:T(8,128)} %bitcast.15, s32[64,128]{1,0:T(8,128)} %bitcast.16, s32[64,128]{1,0:T(8,128)} %bitcast.17, s32[8,128]{1,0:T(8,128)} %bitcast.18, s32[8,128]{1,0:T(8,128)} %bitcast.19, ...), custom_call_target="tpu_custom_call" | custom-call | tf_op jit(solution)/shard_map/route/pallas_call | solution.py:253
  7.6 7.3 %all-to-all-start = ((s32[32,1,768]{2,1,0:T(1,128)}), s32[32,1,768]{2,1,0:T(1,128)S(1)}, u32[]{:S(2)}, u32[]{:S(2)}) async-start(s32[32,1,768]{2,1,0:T(1,128)} %get-tuple-element.6), calls=%async_computation | async-start | bytes 196608 | tf_op jit(solution)/shard_map/all_to_all | solution.py:261
  14.9 7.8 %all-to-all-done.msg = s32[32,1,768]{2,1,0:T(1,128)S(1)} async-done(((s32[32,1,768]{2,1,0:T(1,128)}), s32[32,1,768]{2,1,0:T(1,128)S(1)}, u32[]{:S(2)}, u32[]{:S(2)}) %all-to-all-start) | async-done | bytes 98336 | tf_op jit(solution)/shard_map/all_to_all | solution.py:261
  22.7 15.9 %march.1 = f32[32,1,1536]{2,1,0:T(1,128)S(1)} custom-call(s32[1]{0:T(128)} %bitcast.base, s32[32,1,768]{2,1,0:T(1,128)S(1)} %all-to-all-done.msg, f32[512,128]{1,0:T(8,128)} %fdens.1, f32[512,128]{1,0:T(8,128)} %femis.1, f32[512,128]{1,0:T(8,128)} %cdens.1, f32[512,128]{1,0:T(8,128)} %cemis.1), custom_call_target="tpu_custom_call" | custom-call | tf_op jit(solution)/shard_map/march/pallas_call | solution.py:265
  38.7 10.7 %all_to_all.15.back = f32[32,1,1536]{2,1,0:T(1,128)S(1)} all-to-all(f32[32,1,1536]{2,1,0:T(1,128)S(1)} %march.1), channel_id=1, replica_groups=mesh['morton'=8,'level'=4] {'morton','level'}, dimensions={0} | all-to-all | bytes 393216 | tf_op jit(solution)/shard_map/all_to_all | solution.py:276
  49.3 3.9 %blend.1 = f32[4,1,512]{2,1,0:T(1,128)S(1)} custom-call(f32[32,1,1536]{2,1,0:T(1,128)S(1)} %all_to_all.15.back, s32[64,128]{1,0:T(8,128)} %bitcast.13, s32[16,512]{1,0:T(8,128)} %get-tuple-element.7.ranks), custom_call_target="tpu_custom_call" | custom-call | tf_op jit(solution)/shard_map/blend/pallas_call | solution.py:279
  53.2 6.2 %all_to_all.16.slabs = f32[4,1,512]{2,1,0:T(1,128)S(1)} all-to-all(f32[4,1,512]{2,1,0:T(1,128)S(1)} %blend.1), channel_id=1, replica_groups=mesh['morton'=8,'level'=4] {'level'}, dimensions={0} | all-to-all | bytes 16384 | tf_op jit(solution)/shard_map/all_to_all | solution.py:285
  59.4 0.6 finish.1
Async XLA Ops:
  7.6 15.1 %all-to-all-start = ((s32[32,1,768]{2,1,0:T(1,128)}), s32[32,1,768]{2,1,0:T(1,128)S(1)}, u32[]{:S(2)}, u32[]{:S(2)}) async-start(s32[32,1,768]{2,1,0:T(1,128)} %get-tuple-element.6), calls=%async_computation | async-start | bytes 196608 | tf_op jit(solution)/shard_map/all_to_all | solution.py:261
